TPU v7x, 256 devices: a whole 4x4x8 slice. The times are simulated.
256 devices in a mesh: engine: 4 (over y), ep: 64 (over x, z, core).
Axes of the slice: x: 4, y: 4, z: 8, core: 2. Of those that a mesh axis runs over, the one named last changes fastest.
Arguments:
- tokens: bfloat16 [2, 2048, 4096], P(None, ('engine', 'ep')), may hold values from -6 to 6
- route_ids: int32 [2, 2048, 8], P(None, ('engine', 'ep')), may hold values from 0 to 63, all different within a row; in each aligned block of 8 rows (0 to 7, 8 to 15, ..., all dimensions but the last counted through in order) at most 2 rows name the same one
- route_weights: float32 [2, 2048, 8], P(None, ('engine', 'ep')), may hold values from 0.05 to 1
- placement: int32 [64], replicated, may hold values from 0 to 63, each once
- expert_in: bfloat16 [64, 2, 4096, 1536], P(None, None, ('engine', 'ep')), may hold values from -0.09375 to 0.09375
- expert_down: bfloat16 [64, 1536, 4096], P(None, None, ('engine', 'ep')), may hold values from -0.15625 to 0.15625
Outputs:
- combined: bfloat16 [2, 2048, 4096], P(None, ('engine', 'ep'))
- in_scales: float32 [64, 2, 1536], P('ep', None, 'engine')
- out_scales: float32 [64, 4096], P('ep', 'engine')
Inputs may be any that keep to these rules, and one draw needn't show every extreme that they name: `route_ids`: within the rows of one device in one step no expert is named more than 2 times, a bound that some block reaches. `placement`: each slot holds exactly one expert.
All inputs are finite; a program needn't handle non-finite values.
Results may differ from a plain program's by a relative error of at most 0.0057.
Values may be sent and summed in bfloat16 or wider, within the bound.
A program may use at most 128 MiB of HBM per device.

v0:
```python
import jax
import jax.numpy as jnp
from jax import lax
from jax.sharding import PartitionSpec as P

EPSILON = 1e-06
quant_levels = 31.0


def in_blocks(shard, dim, peers):
    lengths = shard.shape
    parts = shard.reshape(*lengths[:dim], peers, lengths[dim] // peers, *lengths[dim + 1 :])
    return jnp.moveaxis(parts, dim, 0)


def in_order(parts, dim):
    lengths = list(parts.shape[1:])
    lengths[dim] *= parts.shape[0]
    return jnp.moveaxis(parts, 0, dim).reshape(lengths)


def one_exchange(shard, axis, axes, splits, concats):
    sizes = [lax.axis_size(a) for a in axes]
    parts = in_blocks(shard, splits[0], sizes[0])
    parts = jnp.moveaxis(in_blocks(parts, splits[1] + 1, sizes[1]), 0, 1)
    inside = parts.shape[2:]
    parts = parts.reshape(-1, *inside)
    parts = lax.all_to_all(parts, axis, split_axis=0, concat_axis=0, tiled=True)
    parts = in_order(parts.reshape(*sizes, *inside), concats[0] + 1)
    return in_order(parts, concats[1])


def slot_targets(picked, placement, capacity):
    experts = placement.shape[0]
    numbers = jnp.arange(experts, dtype=jnp.int32)
    slot_ids = jnp.sum(jnp.where(picked[..., None] == numbers, placement, 0), axis=-1)
    flat_slots = slot_ids.reshape(-1)
    marked = (flat_slots[:, None] == numbers[None, :]).astype(jnp.int32)
    before = jnp.cumsum(marked, axis=0) - marked
    positions = jnp.sum(before * marked, axis=1)
    return (flat_slots * capacity + positions).reshape(slot_ids.shape)


def pack_rows(local_rows, targets, lane_count):
    lane_ids = jnp.arange(lane_count, dtype=jnp.int32)
    selector = jnp.sum((targets[None, :, :] == lane_ids[:, None, None]).astype(jnp.int32), axis=2)
    return jnp.dot(
        selector.astype(jnp.bfloat16), local_rows, preferred_element_type=jnp.float32
    ).astype(jnp.bfloat16)


def shards(tokens, route_ids, route_weights, placement, expert_in, expert_down):
    experts = placement.shape[0]
    numbers = jnp.arange(experts, dtype=jnp.int32)
    owners = jnp.sum(jnp.where(placement[None, :] == numbers[:, None], numbers[None, :], 0), axis=1)
    sorted_in = jnp.take(expert_in, owners, axis=0)
    sorted_down = jnp.take(expert_down, owners, axis=0)
    engines = lax.axis_size("engine")
    peer_count = lax.axis_size("ep")
    quarter_in, held_down = (
        lax.all_to_all(sorted_in, "ep", split_axis=0, concat_axis=2, tiled=True),
        lax.all_to_all(sorted_down, "ep", split_axis=0, concat_axis=2, tiled=True),
    )
    held_in = lax.all_to_all(quarter_in, "engine", split_axis=3, concat_axis=2, tiled=True)
    scale_in = (jnp.max(jnp.abs(held_in.astype(jnp.float32)), axis=2) + EPSILON) / quant_levels
    quant_in = jnp.floor(held_in.astype(jnp.float32) / scale_in[:, :, None, :] + 0.5).astype(
        jnp.bfloat16
    )
    scale_out = (jnp.max(jnp.abs(held_down.astype(jnp.float32)), axis=1) + EPSILON) / quant_levels
    quant_down = jnp.floor(held_down.astype(jnp.float32) / scale_out[:, None, :] + 0.5).astype(
        jnp.bfloat16
    )
    held_count = quant_in.shape[0]
    row_count = tokens.shape[1]
    top_count = route_ids.shape[2]
    capacity = max(2, (row_count * top_count + experts - 1) // experts)
    lane_count = experts * capacity
    results = []
    for step_index in range(tokens.shape[0]):
        local_rows = tokens[step_index]
        picked = route_ids[step_index]
        targets = slot_targets(picked, placement, capacity)
        packed = pack_rows(local_rows, targets, lane_count).reshape(experts, capacity, -1)
        arrived = lax.all_to_all(packed, "ep", split_axis=0, concat_axis=1, tiled=True)
        arrived = arrived.reshape(held_count, peer_count, capacity, -1)
        projected = jnp.einsum(
            "xpnd,xmdf->xmpnf",
            lax.all_gather(arrived, "engine", axis=2, tiled=True),
            quant_in,
            preferred_element_type=jnp.float32,
        )
        projected = projected * scale_in[:, :, None, None, :]
        hidden = (jax.nn.silu(projected[:, 0]) * projected[:, 1]).astype(jnp.bfloat16)
        summed = jnp.einsum(
            "xpcj,xjd->xpcd",
            lax.all_gather(hidden, "engine", axis=3, tiled=True),
            quant_down,
            preferred_element_type=jnp.float32,
        )
        outcome = (summed * scale_out[:, None, None, :]).astype(jnp.bfloat16)
        outcome = outcome.reshape(held_count, peer_count, engines, capacity, -1)
        returned = one_exchange(outcome, ("engine", "ep"), ("engine", "ep"), (2, 1), (4, 0))
        returned = returned.reshape(lane_count, -1)
        lane_ids = jnp.arange(lane_count, dtype=jnp.int32)
        mixing = jnp.sum(
            jnp.where(targets[:, :, None] == lane_ids, route_weights[step_index][:, :, None], 0.0),
            axis=1,
        )
        merged = jnp.dot(mixing, returned.astype(jnp.float32), precision=lax.Precision.HIGHEST)
        results.append(merged.astype(jnp.bfloat16))
    return (jnp.stack(results), scale_in, scale_out)


def solution(mesh):
    placed = (
        P(None, ("engine", "ep"), None),
        P(None, ("engine", "ep"), None),
        P(None, ("engine", "ep"), None),
        P(),
        P(None, None, ("engine", "ep"), None),
        P(None, None, ("engine", "ep")),
    )
    return jax.shard_map(
        shards,
        mesh=mesh,
        in_specs=placed,
        out_specs=(P(None, ("engine", "ep"), None), P("ep", None, "engine"), P("ep", "engine")),
        check_vma=False,
    )
```

profile of v0, /device:TPU:1, one launch (start us, length us, event | category | flops | bytes accessed | tf_op | source)
XLA Modules:
  0.0 534.4 jit_solution(12656317761184367620)
XLA Ops:
  7.2 0.9 slice_bitcast_fusion.5
  8.1 1.2 select_reduce_fusion.6
  9.9 2.3 convolution_convert_fusion
  12.2 2.5 reshape.356
  14.8 13.2 %all-to-all-start.5 = ((bf16[64,2,4096]{2,1,0:T(2,128)(2,1)}), bf16[64,2,4096]{2,1,0:T(2,128)(2,1)}, u32[]{:S(2)}, u32[]{:S(2)}) async-start(bf16[64,2,4096]{2,1,0:T(2,128)(2,1)} %reshape.356), calls=%async_computation.5 | async-start | bytes 2097152 | tf_op jit(solution)/shard_map/all_to_all | solution.py:84
  28.1 6.4 %gather_fusion = bf16[64,2,16,1536]{3,2,1,0:T(8,128)(2,1)} fusion(bf16[64,2,16,1536]{3,2,1,0:T(8,128)(2,1)} %param.10, s32[1024]{0:T(1024)S(1)} %pad_clamp_fusion), kind=kCustom, calls=%fused_computation | custom fusion | bytes 12583168 | tf_op jit(solution)/shard_map/jit(_take)/gather | solution.py:56
  34.5 6.1 %broadcast_select_fusion = bf16[64,2,16,1536]{3,2,1,0:T(8,128)(2,1)} fusion(bf16[64,2,16,1536]{3,2,1,0:T(8,128)(2,1)} %gather_fusion, pred[64]{0:T(512)(128)(4,1)S(1)} %compare_and_fusion), kind=kLoop, calls=%fused_computation.15 | loop fusion | flops 3145728 | bytes 12582976 | tf_op jit(solution)/shard_map/jit(_take)/select_n | solution.py:56
  40.6 15.8 %all-to-all-done.5 = bf16[64,2,4096]{2,1,0:T(2,128)(2,1)} async-done(((bf16[64,2,4096]{2,1,0:T(2,128)(2,1)}), bf16[64,2,4096]{2,1,0:T(2,128)(2,1)}, u32[]{:S(2)}, u32[]{:S(2)}) %all-to-all-start.5) | async-done | bytes 1048608 | tf_op jit(solution)/shard_map/all_to_all | solution.py:84
  56.4 6.4 %all-to-all-start = ((bf16[64,2,16,1536]{3,2,1,0:T(8,128)(2,1)}), bf16[64,2,16,1536]{3,2,1,0:T(8,128)(2,1)}, u32[]{:S(2)}, u32[]{:S(2)}) async-start(bf16[64,2,16,1536]{3,2,1,0:T(8,128)(2,1)} %broadcast_select_fusion), calls=%async_computation | async-start | bytes 12582912 | tf_op jit(solution)/shard_map/all_to_all | solution.py:61
  63.4 2.8 copy.65
  66.2 1.5 convolution_convert_fusion.1
  67.7 2.6 reshape.351
  70.3 133.3 %all-to-all-done = bf16[64,2,16,1536]{3,2,1,0:T(8,128)(2,1)} async-done(((bf16[64,2,16,1536]{3,2,1,0:T(8,128)(2,1)}), bf16[64,2,16,1536]{3,2,1,0:T(8,128)(2,1)}, u32[]{:S(2)}, u32[]{:S(2)}) %all-to-all-start) | async-done | bytes 6291488 | tf_op jit(solution)/shard_map/all_to_all | solution.py:61
  203.6 6.0 %all-to-all-start.2 = ((bf16[64,2,4096]{2,1,0:T(2,128)(2,1)}), bf16[64,2,4096]{2,1,0:T(2,128)(2,1)}, u32[]{:S(2)}, u32[]{:S(2)}) async-start(bf16[64,2,4096]{2,1,0:T(2,128)(2,1)} %reshape.351), calls=%async_computation.2 | async-start | bytes 2097152 | tf_op jit(solution)/shard_map/all_to_all | solution.py:84
  209.5 6.0 %copy.55 = bf16[1,2,64,16,1536]{4,3,2,1,0:T(8,128)(2,1)} copy(bf16[1,2,64,16,1536]{4,3,1,2,0:T(8,128)(2,1)} %bitcast.5) | data formatting | bytes 12582912 | tf_op jit(solution)/shard_map/all_to_all | solution.py:61
  215.5 16.4 %copy.56 = bf16[1,2,1024,1536]{2,1,0,3:T(2,128)(2,1)} copy(bf16[1,2,1024,1536]{3,2,1,0:T(8,128)(2,1)} %bitcast.119) | data formatting | bytes 12582912 | tf_op jit(solution)/shard_map/all_to_all | solution.py:61
  231.9 6.1 %all-to-all-done.2 = bf16[64,2,4096]{2,1,0:T(2,128)(2,1)} async-done(((bf16[64,2,4096]{2,1,0:T(2,128)(2,1)}), bf16[64,2,4096]{2,1,0:T(2,128)(2,1)}, u32[]{:S(2)}, u32[]{:S(2)}) %all-to-all-start.2) | async-done | bytes 1048608 | tf_op jit(solution)/shard_map/all_to_all | solution.py:84
  238.0 5.2 all-to-all-start.1
  243.3 2.4 gather_fusion.1
  245.7 3.0 copy.59
  248.8 2.0 broadcast_select_fusion.1
  250.8 97.5 %all-to-all-done.1 = bf16[1,2,1024,1536]{2,1,0,3:T(2,128)(2,1)} async-done(((bf16[1,2,1024,1536]{2,1,0,3:T(2,128)(2,1)}), bf16[1,2,1024,1536]{2,1,0,3:T(2,128)(2,1)}, u32[]{:S(2)}, u32[]{:S(2)}) %all-to-all-start.1) | async-done | bytes 6291488 | tf_op jit(solution)/shard_map/all_to_all | solution.py:64
  348.3 6.6 %all-to-all-start.3 = ((bf16[64,1536,16]{1,2,0:T(8,128)(2,1)}), bf16[64,1536,16]{1,2,0:T(8,128)(2,1)S(1)}, u32[]{:S(2)}, u32[]{:S(2)}) async-start(bf16[64,1536,16]{1,2,0:T(8,128)(2,1)} %broadcast_select_fusion.1), calls=%async_computation.3 | async-start | bytes 6291456 | tf_op jit(solution)/shard_map/all_to_all | solution.py:62
  355.1 4.8 copy.57
  359.9 1.6 fusion
  362.1 4.2 fusion.8
  366.3 8.7 %copy.58 = bf16[1,2,4,1024,384]{4,3,2,1,0:T(8,128)(2,1)} copy(bf16[1,2,4,1024,384]{3,4,2,1,0:T(8,128)(2,1)} %fusion.8) | data formatting | bytes 12582912 | tf_op jit(solution)/shard_map/floor | solution.py:66
  374.9 7.1 %fusion.15 = f32[1,2,64,8,384]{4,2,3,1,0:T(8,128)S(1)} fusion(bf16[2,4096,384,1]{2,1,3,0:T(8,128)(2,1)} %bitcast.120, bf16[64,8,4096]{2,0,1:T(8,128)(2,1)} %all-gather.13.cloned.1.call-done, f32[2,384]{1,0:T(2,128)S(1)} %get-tuple-element.10), kind=kOutput, calls=%fused_computation.30 | convolution fusion | flops 3221618688 | bytes 12061696 | tf_op jit(solution)/shard_map/xpnd,xmdf->xmpnf/dot_general | solution.py:86
  382.1 1.0 fusion.24
  383.3 45.0 %all-to-all-done.3 = bf16[64,1536,16]{1,2,0:T(8,128)(2,1)S(1)} async-done(((bf16[64,1536,16]{1,2,0:T(8,128)(2,1)}), bf16[64,1536,16]{1,2,0:T(8,128)(2,1)S(1)}, u32[]{:S(2)}, u32[]{:S(2)}) %all-to-all-start.3) | async-done | bytes 3145760 | tf_op jit(solution)/shard_map/all_to_all | solution.py:62
  428.3 0.7 fusion.4
  429.0 7.1 %fusion.16 = f32[1,2,64,8,384]{4,2,3,1,0:T(8,128)S(1)} fusion(bf16[2,4096,384,1]{2,1,3,0:T(8,128)(2,1)} %bitcast.121, bf16[64,8,4096]{2,0,1:T(8,128)(2,1)} %all-gather.11.cloned.1.call-done, f32[2,384]{1,0:T(2,128)S(1)} %get-tuple-element.10), kind=kOutput, calls=%fused_computation.32 | convolution fusion | flops 3221618688 | bytes 12061696 | tf_op jit(solution)/shard_map/xpnd,xmdf->xmpnf/dot_general | solution.py:86
  436.2 1.0 fusion.26
  437.2 2.4 fusion.7
  439.6 4.4 multiply_convert_fusion
  445.0 2.1 copy.69
  447.1 6.4 %all-to-all-start.6 = ((bf16[256,1,1,1,2,1024]{5,4,3,2,1,0:T(2,128)(2,1)}), bf16[256,1,1,1,2,1024]{5,4,3,2,1,0:T(2,128)(2,1)S(1)}, u32[]{:S(2)}, u32[]{:S(2)}) async-start(bf16[256,1,1,1,2,1024]{5,4,3,2,1,0:T(2,128)(2,1)} %copy.69), calls=%async_computation.6 | async-start | bytes 2097152 | tf_op jit(solution)/shard_map/all_to_all | solution.py:28
  453.5 9.7 %all-gather.7.cloned.1.call-done = bf16[1,64,8,1536]{3,1,2,0:T(8,128)(2,1)} async-done(((bf16[1,64,8,384]{3,1,2,0:T(8,128)(2,1)}), bf16[1,64,8,1536]{3,1,2,0:T(8,128)(2,1)}) %all-gather.7.cloned.1.call-update) | async-done | bytes 1572880 | tf_op jit(solution)/shard_map/all_gather | solution.py:96
  463.2 4.4 multiply_convert_fusion.1
  468.6 2.1 copy.63
  470.7 15.3 %all-to-all-done.6 = bf16[256,1,1,1,2,1024]{5,4,3,2,1,0:T(2,128)(2,1)S(1)} async-done(((bf16[256,1,1,1,2,1024]{5,4,3,2,1,0:T(2,128)(2,1)}), bf16[256,1,1,1,2,1024]{5,4,3,2,1,0:T(2,128)(2,1)S(1)}, u32[]{:S(2)}, u32[]{:S(2)}) %all-to-all-start.6) | async-done | bytes 1048608 | tf_op jit(solution)/shard_map/all_to_all | solution.py:28
  485.9 6.8 %all-to-all-start.4 = ((bf16[256,1,1,1,2,1024]{5,4,3,2,1,0:T(2,128)(2,1)}), bf16[256,1,1,1,2,1024]{5,4,3,2,1,0:T(2,128)(2,1)}, u32[]{:S(2)}, u32[]{:S(2)}) async-start(bf16[256,1,1,1,2,1024]{5,4,3,2,1,0:T(2,128)(2,1)} %copy.63), calls=%async_computation.4 | async-start | bytes 2097152 | tf_op jit(solution)/shard_map/all_to_all | solution.py:28
  492.9 0.7 div.85
  493.6 1.4 copy.70
  495.0 1.4 copy.77
  496.3 26.8 %all-to-all-done.4 = bf16[256,1,1,1,2,1024]{5,4,3,2,1,0:T(2,128)(2,1)} async-done(((bf16[256,1,1,1,2,1024]{5,4,3,2,1,0:T(2,128)(2,1)}), bf16[256,1,1,1,2,1024]{5,4,3,2,1,0:T(2,128)(2,1)}, u32[]{:S(2)}, u32[]{:S(2)}) %all-to-all-start.4) | async-done | bytes 1048608 | tf_op jit(solution)/shard_map/all_to_all | solution.py:28
  523.1 2.7 copy.64
  527.2 0.7 pad_maximum_fusion
  (55 shorter events, 6.3 us)
Async XLA Ops:
  7.2 236.1 %copy-start = (bf16[64,1536,16]{1,2,0:T(8,128)(2,1)S(1)}, bf16[64,1536,16]{1,2,0:T(8,128)(2,1)}, u32[]{:S(2)}) copy-start(bf16[64,1536,16]{1,2,0:T(8,128)(2,1)} %param.11) | copy-start | bytes 9437188
  7.2 20.8 %copy-start.6 = (s32[64]{0:T(128)S(1)}, s32[64]{0:T(128)}, u32[]{:S(2)}) copy-start(s32[64]{0:T(128)} %param.9) | copy-start | bytes 772
  14.8 41.6 %all-to-all-start.5 = ((bf16[64,2,4096]{2,1,0:T(2,128)(2,1)}), bf16[64,2,4096]{2,1,0:T(2,128)(2,1)}, u32[]{:S(2)}, u32[]{:S(2)}) async-start(bf16[64,2,4096]{2,1,0:T(2,128)(2,1)} %reshape.356), calls=%async_computation.5 | async-start | bytes 2097152 | tf_op jit(solution)/shard_map/all_to_all | solution.py:84
  40.6 25.7 %copy-start.4 = (bf16[2,8,4096]{2,1,0:T(8,128)(2,1)S(1)}, bf16[2,8,4096]{2,1,0:T(8,128)(2,1)}, u32[]{:S(2)}) copy-start(bf16[2,8,4096]{2,1,0:T(8,128)(2,1)} %param.6) | copy-start | bytes 393220
  56.4 147.2 %all-to-all-start = ((bf16[64,2,16,1536]{3,2,1,0:T(8,128)(2,1)}), bf16[64,2,16,1536]{3,2,1,0:T(8,128)(2,1)}, u32[]{:S(2)}, u32[]{:S(2)}) async-start(bf16[64,2,16,1536]{3,2,1,0:T(8,128)(2,1)} %broadcast_select_fusion), calls=%async_computation | async-start | bytes 12582912 | tf_op jit(solution)/shard_map/all_to_all | solution.py:61
  62.7 312.2 %all-gather.13.cloned.1.call-start = ((), (), s32[]{:S(2)}) async-start(), calls=%async_computation.10 | async-start | bytes 5242880 | tf_op jit(solution)/shard_map/all_gather | solution.py:88
  203.6 34.4 %all-to-all-start.2 = ((bf16[64,2,4096]{2,1,0:T(2,128)(2,1)}), bf16[64,2,4096]{2,1,0:T(2,128)(2,1)}, u32[]{:S(2)}, u32[]{:S(2)}) async-start(bf16[64,2,4096]{2,1,0:T(2,128)(2,1)} %reshape.351), calls=%async_computation.2 | async-start | bytes 2097152 | tf_op jit(solution)/shard_map/all_to_all | solution.py:84
  238.0 110.3 %all-to-all-start.1 = ((bf16[1,2,1024,1536]{2,1,0,3:T(2,128)(2,1)}), bf16[1,2,1024,1536]{2,1,0,3:T(2,128)(2,1)}, u32[]{:S(2)}, u32[]{:S(2)}) async-start(bf16[1,2,1024,1536]{2,1,0,3:T(2,128)(2,1)} %copy.56), calls=%async_computation.1 | async-start | bytes 12582912 | tf_op jit(solution)/shard_map/all_to_all | solution.py:64
  243.2 185.8 %all-gather.11.cloned.1.call-start = ((), (), s32[]{:S(2)}) async-start(), calls=%async_computation.9 | async-start | bytes 5242880 | tf_op jit(solution)/shard_map/all_gather | solution.py:88
  245.7 3.1 copy-start.2
  348.3 80.0 %all-to-all-start.3 = ((bf16[64,1536,16]{1,2,0:T(8,128)(2,1)}), bf16[64,1536,16]{1,2,0:T(8,128)(2,1)S(1)}, u32[]{:S(2)}, u32[]{:S(2)}) async-start(bf16[64,1536,16]{1,2,0:T(8,128)(2,1)} %broadcast_select_fusion.1), calls=%async_computation.3 | async-start | bytes 6291456 | tf_op jit(solution)/shard_map/all_to_all | solution.py:62
  354.9 84.8 %all-gather.9.cloned.1.call-start = ((), (), s32[]{:S(2)}) async-start(), calls=%async_computation.8 | async-start | bytes 1966080 | tf_op jit(solution)/shard_map/all_gather | solution.py:96
  383.1 80.2 %all-gather.7.cloned.1.call-start = ((), (), s32[]{:S(2)}) async-start(), calls=%async_computation.7 | async-start | bytes 1966080 | tf_op jit(solution)/shard_map/all_gather | solution.py:96
  447.1 38.8 %all-to-all-start.6 = ((bf16[256,1,1,1,2,1024]{5,4,3,2,1,0:T(2,128)(2,1)}), bf16[256,1,1,1,2,1024]{5,4,3,2,1,0:T(2,128)(2,1)S(1)}, u32[]{:S(2)}, u32[]{:S(2)}) async-start(bf16[256,1,1,1,2,1024]{5,4,3,2,1,0:T(2,128)(2,1)} %copy.69), calls=%async_computation.6 | async-start | bytes 2097152 | tf_op jit(solution)/shard_map/all_to_all | solution.py:28
  467.6 25.2 %copy-start.5 = (f32[2,8,8]{2,1,0:T(8,128)S(1)}, f32[2,8,8]{2,1,0:T(8,128)}, u32[]{:S(2)}) copy-start(f32[2,8,8]{2,1,0:T(8,128)} %param.8) | copy-start | bytes 1540
  485.9 37.2 %all-to-all-start.4 = ((bf16[256,1,1,1,2,1024]{5,4,3,2,1,0:T(2,128)(2,1)}), bf16[256,1,1,1,2,1024]{5,4,3,2,1,0:T(2,128)(2,1)}, u32[]{:S(2)}, u32[]{:S(2)}) async-start(bf16[256,1,1,1,2,1024]{5,4,3,2,1,0:T(2,128)(2,1)} %copy.63), calls=%async_computation.4 | async-start | bytes 2097152 | tf_op jit(solution)/shard_map/all_to_all | solution.py:28
  495.0 32.9 %copy-start.1 = (bf16[64,1536,16]{1,2,0:T(8,128)(2,1)S(1)}, bf16[64,1536,16]{1,2,0:T(8,128)(2,1)}, u32[]{:S(2)}) copy-start(bf16[64,1536,16]{1,2,0:T(8,128)(2,1)} %param.11) | copy-start | bytes 9437188
  523.1 3.1 copy-start.3
Sparse Core Ops, SparseCore 0:
  66.4 51.7 all-gather.12
  248.9 81.6 all-gather.10
  383.2 27.9 all-gather.8
  437.3 25.8 all-gather.6
where the time goes:
time: 536 us; the launch traced here: 534 us
  waiting for transfers between devices  349 us (65%)
  local copies, waits for them, and re-layouts  69.4 us (13%)
  starting transfers between devices  51.1 us (10%)
  matrix products  27.8 us (5%)
  other arithmetic  22.6 us (4%)
  between operations  14.1 us (3%)
    all_to_all x1, waiting for transfers between devices, shards(): lax.all_to_all(sorted_in, 'ep', split_axis=0, concat_axis=2, tiled=True)  133 us
    all_to_all x1, waiting for transfers between devices, shards(): lax.all_to_all(quarter_in, 'engine', split_axis=3, concat_axis=2, tiled=T...  97.5 us
    all_to_all x1, waiting for transfers between devices, shards(): lax.all_to_all(sorted_down, 'ep', split_axis=0, concat_axis=2, tiled=True)  45 us
    all_to_all x2, waiting for transfers between devices, one_exchange(): parts = lax.all_to_all(parts, axis, split_axis=0, concat_axis=0, tiled=True)  42 us
    all_to_all x2, local copies, waits for them, and re-layouts, shards(): lax.all_to_all(sorted_in, 'ep', split_axis=0, concat_axis=2, tiled=True)  22.3 us
    all_to_all x2, waiting for transfers between devices, shards(): lax.all_to_all(packed, 'ep', split_axis=0, concat_axis=1, tiled=True)  21.9 us
    all_to_all x2, starting transfers between devices, shards(): lax.all_to_all(packed, 'ep', split_axis=0, concat_axis=1, tiled=True)  19.1 us
    dot_general x2, matrix products, shards(): jnp.einsum('xpnd,xmdf->xmpnf', lax.all_gather(arrived, 'engine', axis=2,...  14.2 us
  transfers between devices with their start and end apart: 11, of which 8 were waited for; matrix products, arithmetic and copies ran while one was open for 20% of the time, Pallas kernels for 0%

commit v1 on v0

--- a/solution.py
+++ b/solution.py
@@ -58,7 +58,12 @@
     engines = lax.axis_size("engine")
     peer_count = lax.axis_size("ep")
     quarter_in, held_down = (
-        lax.all_to_all(sorted_in, "ep", split_axis=0, concat_axis=2, tiled=True),
+        jnp.concatenate(
+            lax.all_to_all(
+                jnp.stack(jnp.split(sorted_in, lax.axis_size("ep"), axis=0)), "ep", 0, 0
+            ),
+            axis=2,
+        ),
         lax.all_to_all(sorted_down, "ep", split_axis=0, concat_axis=2, tiled=True),
     )
     held_in = lax.all_to_all(quarter_in, "engine", split_axis=3, concat_axis=2, tiled=True)

time: 536 us -> 565 us (1.054)
  local copies, waits for them, and re-layouts: 69.4 us -> 111 us
  waiting for transfers between devices: 349 us -> 330 us
    unnamed x16 -> x73, local copies, waits for them, and re-layouts: 1.77 us -> 42.2 us
    all_to_all x2 -> x1, local copies, waits for them, and re-layouts: 22.3 us -> 5.98 us  [shards(): lax.all_to_all(jnp.stack(jnp.split(sorted_in, lax.axis_size('ep'), axis=0...]
    reshape x0 -> x1, local copies, waits for them, and re-layouts: none -> 16.4 us  [shards(): jnp.concatenate(lax.all_to_all(jnp.stack(jnp.split(sorted_in, lax.axis_si...]
    all_to_all x2, waiting for transfers between devices: 21.9 us -> 6.09 us  [shards(): lax.all_to_all(packed, 'ep', split_axis=0, concat_axis=1, tiled=True)]
  transfers between devices with their start and end apart: 11 -> 11, of which waited for: 8 -> 7; matrix products, arithmetic and copies ran while one was open for 20% -> 27% of each run, Pallas kernels for 0% -> 0%
where the time goes in v1:
time: 565 us; the launch traced here: 563 us
  waiting for transfers between devices  330 us (58%)
  local copies, waits for them, and re-layouts  111 us (20%)
  starting transfers between devices  56.4 us (10%)
  matrix products  29 us (5%)
  other arithmetic  22.5 us (4%)
  between operations  14.1 us (2%)
    all_to_all x1, waiting for transfers between devices, shards(): lax.all_to_all(jnp.stack(jnp.split(sorted_in, lax.axis_size('ep'), axis=0...  133 us
    all_to_all x1, waiting for transfers between devices, shards(): lax.all_to_all(quarter_in, 'engine', split_axis=3, concat_axis=2, tiled=T...  95.8 us
    all_to_all x1, waiting for transfers between devices, shards(): lax.all_to_all(sorted_down, 'ep', split_axis=0, concat_axis=2, tiled=True)  45 us
    unnamed x73, local copies, waits for them, and re-layouts  42.2 us
    all_to_all x2, waiting for transfers between devices, one_exchange(): parts = lax.all_to_all(parts, axis, split_axis=0, concat_axis=0, tiled=True)  40.9 us
    all_to_all x2, starting transfers between devices, shards(): lax.all_to_all(packed, 'ep', split_axis=0, concat_axis=1, tiled=True)  19.1 us
    reshape x1, local copies, waits for them, and re-layouts, shards(): jnp.concatenate(lax.all_to_all(jnp.stack(jnp.split(sorted_in, lax.axis_si...  16.4 us
    all_to_all x2, starting transfers between devices, one_exchange(): parts = lax.all_to_all(parts, axis, split_axis=0, concat_axis=0, tiled=True)  14.2 us
  transfers between devices with their start and end apart: 11, of which 7 were waited for; matrix products, arithmetic and copies ran while one was open for 27% of the time, Pallas kernels for 0%

profile of v1, /device:TPU:1, one launch (start us, length us, event | category | flops | bytes accessed | tf_op | source)
XLA Modules:
  0.0 563.1 jit_solution(16995164316896863729)
XLA Ops:
  7.2 0.9 slice_bitcast_fusion.69
  8.0 1.2 select_reduce_fusion.6
  9.9 2.3 convolution_convert_fusion.1
  12.2 2.5 reshape.359
  14.7 13.2 %all-to-all-start.2 = ((bf16[64,2,4096]{2,1,0:T(2,128)(2,1)}), bf16[64,2,4096]{2,1,0:T(2,128)(2,1)}, u32[]{:S(2)}, u32[]{:S(2)}) async-start(bf16[64,2,4096]{2,1,0:T(2,128)(2,1)} %reshape.359), calls=%async_computation.2 | async-start | bytes 2097152 | tf_op jit(solution)/shard_map/all_to_all | solution.py:89
  27.9 0.8 select_reduce_fusion.3
  28.7 6.4 %gather_fusion = bf16[64,2,16,1536]{3,2,1,0:T(8,128)(2,1)} fusion(bf16[64,2,16,1536]{3,2,1,0:T(8,128)(2,1)} %param.10, s32[1024]{0:T(1024)S(1)} %pad_clamp_fusion), kind=kCustom, calls=%fused_computation | custom fusion | bytes 12583168 | tf_op jit(solution)/shard_map/jit(_take)/gather | solution.py:56
  35.1 3.4 broadcast_select_fusion
  79.6 10.6 %all-to-all-start = ((bf16[64,1,2,16,1536]{4,3,2,1,0:T(8,128)(2,1)}), bf16[64,1,2,16,1536]{4,3,2,1,0:T(8,128)(2,1)}, u32[]{:S(2)}, u32[]{:S(2)}) async-start(bf16[64,1,2,16,1536]{4,3,2,1,0:T(8,128)(2,1)} %constant_dynamic-update-slice_fusion), calls=%async_computation | async-start | bytes 12582912 | tf_op jit(solution)/shard_map/all_to_all | solution.py:62
  90.9 2.8 copy.184
  93.8 1.5 convolution_convert_fusion
  95.2 2.6 reshape.364
  97.8 133.3 %all-to-all-done = bf16[64,1,2,16,1536]{4,3,2,1,0:T(8,128)(2,1)} async-done(((bf16[64,1,2,16,1536]{4,3,2,1,0:T(8,128)(2,1)}), bf16[64,1,2,16,1536]{4,3,2,1,0:T(8,128)(2,1)}, u32[]{:S(2)}, u32[]{:S(2)}) %all-to-all-start) | async-done | bytes 6291488 | tf_op jit(solution)/shard_map/all_to_all | solution.py:62
  231.1 6.0 %all-to-all-start.5 = ((bf16[64,2,4096]{2,1,0:T(2,128)(2,1)}), bf16[64,2,4096]{2,1,0:T(2,128)(2,1)}, u32[]{:S(2)}, u32[]{:S(2)}) async-start(bf16[64,2,4096]{2,1,0:T(2,128)(2,1)} %reshape.364), calls=%async_computation.5 | async-start | bytes 2097152 | tf_op jit(solution)/shard_map/all_to_all | solution.py:89
  237.1 6.0 %copy.180 = bf16[64,1,2,16,1536]{4,3,0,2,1:T(8,128)(2,1)} copy(bf16[64,1,2,16,1536]{4,3,2,1,0:T(8,128)(2,1)} %all-to-all-done) | data formatting | bytes 12582912 | tf_op jit(solution)/shard_map/all_to_all | solution.py:62
  243.0 16.4 %copy.181 = bf16[1,2,1024,1536]{2,1,0,3:T(2,128)(2,1)} copy(bf16[1,2,1024,1536]{3,2,1,0:T(8,128)(2,1)} %bitcast.374) | data formatting | bytes 12582912 | tf_op jit(solution)/shard_map/reshape | solution.py:61
  259.4 6.1 %all-to-all-done.5 = bf16[64,2,4096]{2,1,0:T(2,128)(2,1)} async-done(((bf16[64,2,4096]{2,1,0:T(2,128)(2,1)}), bf16[64,2,4096]{2,1,0:T(2,128)(2,1)}, u32[]{:S(2)}, u32[]{:S(2)}) %all-to-all-start.5) | async-done | bytes 1048608 | tf_op jit(solution)/shard_map/all_to_all | solution.py:89
  265.5 5.2 all-to-all-start.1
  270.8 2.4 gather_fusion.1
  273.2 2.9 copy.190
  276.1 3.9 broadcast_select_fusion.1
  280.0 95.8 %all-to-all-done.1 = bf16[1,2,1024,1536]{2,1,0,3:T(2,128)(2,1)} async-done(((bf16[1,2,1024,1536]{2,1,0,3:T(2,128)(2,1)}), bf16[1,2,1024,1536]{2,1,0,3:T(2,128)(2,1)}, u32[]{:S(2)}, u32[]{:S(2)}) %all-to-all-start.1) | async-done | bytes 6291488 | tf_op jit(solution)/shard_map/all_to_all | solution.py:69
  375.8 6.6 %all-to-all-start.3 = ((bf16[64,1536,16]{1,2,0:T(8,128)(2,1)}), bf16[64,1536,16]{1,2,0:T(8,128)(2,1)S(1)}, u32[]{:S(2)}, u32[]{:S(2)}) async-start(bf16[64,1536,16]{1,2,0:T(8,128)(2,1)} %broadcast_select_fusion.1), calls=%async_computation.3 | async-start | bytes 6291456 | tf_op jit(solution)/shard_map/all_to_all | solution.py:67
  382.6 4.8 copy.182
  387.4 1.6 fusion
  389.6 4.2 fusion.8
  393.8 8.7 %copy.183 = bf16[1,2,4,1024,384]{4,3,2,1,0:T(8,128)(2,1)} copy(bf16[1,2,4,1024,384]{3,4,2,1,0:T(8,128)(2,1)} %fusion.8) | data formatting | bytes 12582912 | tf_op jit(solution)/shard_map/floor | solution.py:71
  402.5 7.1 %fusion.16 = f32[1,2,64,8,384]{4,2,3,1,0:T(8,128)S(1)} fusion(bf16[2,4096,384,1]{2,1,3,0:T(8,128)(2,1)} %bitcast.375, bf16[64,8,4096]{2,0,1:T(8,128)(2,1)} %all-gather.11.cloned.1.call-done, f32[2,384]{1,0:T(2,128)S(1)} %get-tuple-element.10), kind=kOutput, calls=%fused_computation.32 | convolution fusion | flops 3221618688 | bytes 12061696 | tf_op jit(solution)/shard_map/xpnd,xmdf->xmpnf/dot_general | solution.py:91
  409.6 1.0 fusion.26
  410.8 45.0 %all-to-all-done.3 = bf16[64,1536,16]{1,2,0:T(8,128)(2,1)S(1)} async-done(((bf16[64,1536,16]{1,2,0:T(8,128)(2,1)}), bf16[64,1536,16]{1,2,0:T(8,128)(2,1)S(1)}, u32[]{:S(2)}, u32[]{:S(2)}) %all-to-all-start.3) | async-done | bytes 3145760 | tf_op jit(solution)/shard_map/all_to_all | solution.py:67
  456.5 7.1 %fusion.15 = f32[1,2,64,8,384]{4,2,3,1,0:T(8,128)S(1)} fusion(bf16[2,4096,384,1]{2,1,3,0:T(8,128)(2,1)} %bitcast.376, bf16[64,8,4096]{2,0,1:T(8,128)(2,1)} %all-gather.13.cloned.1.call-done, f32[2,384]{1,0:T(2,128)S(1)} %get-tuple-element.10), kind=kOutput, calls=%fused_computation.30 | convolution fusion | flops 3221618688 | bytes 12061696 | tf_op jit(solution)/shard_map/xpnd,xmdf->xmpnf/dot_general | solution.py:91
  463.7 1.0 fusion.24
  464.7 2.4 fusion.7
  467.1 4.3 multiply_convert_fusion.1
  472.5 2.1 copy.188
  474.6 7.4 %all-to-all-start.4 = ((bf16[256,1,1,1,2,1024]{5,4,3,2,1,0:T(2,128)(2,1)}), bf16[256,1,1,1,2,1024]{5,4,3,2,1,0:T(2,128)(2,1)}, u32[]{:S(2)}, u32[]{:S(2)}) async-start(bf16[256,1,1,1,2,1024]{5,4,3,2,1,0:T(2,128)(2,1)} %copy.188), calls=%async_computation.4 | async-start | bytes 2097152 | tf_op jit(solution)/shard_map/all_to_all | solution.py:28
  482.0 8.8 %all-gather.9.cloned.1.call-done = bf16[1,64,8,1536]{3,1,2,0:T(8,128)(2,1)} async-done(((bf16[1,64,8,384]{3,1,2,0:T(8,128)(2,1)}), bf16[1,64,8,1536]{3,1,2,0:T(8,128)(2,1)}) %all-gather.9.cloned.1.call-update) | async-done | bytes 1572880 | tf_op jit(solution)/shard_map/all_gather | solution.py:101
  490.8 4.3 multiply_convert_fusion
  496.2 2.1 copy.194
  498.2 15.3 %all-to-all-done.4 = bf16[256,1,1,1,2,1024]{5,4,3,2,1,0:T(2,128)(2,1)} async-done(((bf16[256,1,1,1,2,1024]{5,4,3,2,1,0:T(2,128)(2,1)}), bf16[256,1,1,1,2,1024]{5,4,3,2,1,0:T(2,128)(2,1)}, u32[]{:S(2)}, u32[]{:S(2)}) %all-to-all-start.4) | async-done | bytes 1048608 | tf_op jit(solution)/shard_map/all_to_all | solution.py:28
  513.5 6.8 %all-to-all-start.6 = ((bf16[256,1,1,1,2,1024]{5,4,3,2,1,0:T(2,128)(2,1)}), bf16[256,1,1,1,2,1024]{5,4,3,2,1,0:T(2,128)(2,1)}, u32[]{:S(2)}, u32[]{:S(2)}) async-start(bf16[256,1,1,1,2,1024]{5,4,3,2,1,0:T(2,128)(2,1)} %copy.194), calls=%async_computation.6 | async-start | bytes 2097152 | tf_op jit(solution)/shard_map/all_to_all | solution.py:28
  520.5 0.7 div.85
  521.2 2.6 copy.189
  523.8 1.4 copy.201
  525.1 25.6 %all-to-all-done.6 = bf16[256,1,1,1,2,1024]{5,4,3,2,1,0:T(2,128)(2,1)} async-done(((bf16[256,1,1,1,2,1024]{5,4,3,2,1,0:T(2,128)(2,1)}), bf16[256,1,1,1,2,1024]{5,4,3,2,1,0:T(2,128)(2,1)}, u32[]{:S(2)}, u32[]{:S(2)}) %all-to-all-start.6) | async-done | bytes 1048608 | tf_op jit(solution)/shard_map/all_to_all | solution.py:28
  550.7 2.6 copy.195
  553.7 1.7 fusion.9
  555.9 0.7 pad_maximum_fusion
  (113 shorter events, 47.4 us)
Async XLA Ops:
  7.2 263.6 %copy-start = (bf16[64,1536,16]{1,2,0:T(8,128)(2,1)S(1)}, bf16[64,1536,16]{1,2,0:T(8,128)(2,1)}, u32[]{:S(2)}) copy-start(bf16[64,1536,16]{1,2,0:T(8,128)(2,1)} %param.11) | copy-start | bytes 9437188
  14.7 64.9 %all-to-all-start.2 = ((bf16[64,2,4096]{2,1,0:T(2,128)(2,1)}), bf16[64,2,4096]{2,1,0:T(2,128)(2,1)}, u32[]{:S(2)}, u32[]{:S(2)}) async-start(bf16[64,2,4096]{2,1,0:T(2,128)(2,1)} %reshape.359), calls=%async_computation.2 | async-start | bytes 2097152 | tf_op jit(solution)/shard_map/all_to_all | solution.py:89
  79.6 14.1 %copy-start.2 = (bf16[2,8,4096]{2,1,0:T(8,128)(2,1)S(1)}, bf16[2,8,4096]{2,1,0:T(8,128)(2,1)}, u32[]{:S(2)}) copy-start(bf16[2,8,4096]{2,1,0:T(8,128)(2,1)} %param.6) | copy-start | bytes 393220
  79.6 151.4 %all-to-all-start = ((bf16[64,1,2,16,1536]{4,3,2,1,0:T(8,128)(2,1)}), bf16[64,1,2,16,1536]{4,3,2,1,0:T(8,128)(2,1)}, u32[]{:S(2)}, u32[]{:S(2)}) async-start(bf16[64,1,2,16,1536]{4,3,2,1,0:T(8,128)(2,1)} %constant_dynamic-update-slice_fusion), calls=%async_computation | async-start | bytes 12582912 | tf_op jit(solution)/shard_map/all_to_all | solution.py:62
  90.3 312.2 %all-gather.11.cloned.1.call-start = ((), (), s32[]{:S(2)}) async-start(), calls=%async_computation.9 | async-start | bytes 5242880 | tf_op jit(solution)/shard_map/all_gather | solution.py:93
  231.1 34.4 %all-to-all-start.5 = ((bf16[64,2,4096]{2,1,0:T(2,128)(2,1)}), bf16[64,2,4096]{2,1,0:T(2,128)(2,1)}, u32[]{:S(2)}, u32[]{:S(2)}) async-start(bf16[64,2,4096]{2,1,0:T(2,128)(2,1)} %reshape.364), calls=%async_computation.5 | async-start | bytes 2097152 | tf_op jit(solution)/shard_map/all_to_all | solution.py:89
  265.5 110.3 %all-to-all-start.1 = ((bf16[1,2,1024,1536]{2,1,0,3:T(2,128)(2,1)}), bf16[1,2,1024,1536]{2,1,0,3:T(2,128)(2,1)}, u32[]{:S(2)}, u32[]{:S(2)}) async-start(bf16[1,2,1024,1536]{2,1,0,3:T(2,128)(2,1)} %copy.181), calls=%async_computation.1 | async-start | bytes 12582912 | tf_op jit(solution)/shard_map/all_to_all | solution.py:69
  270.7 185.8 %all-gather.13.cloned.1.call-start = ((), (), s32[]{:S(2)}) async-start(), calls=%async_computation.10 | async-start | bytes 5242880 | tf_op jit(solution)/shard_map/all_gather | solution.py:93
  375.8 80.0 %all-to-all-start.3 = ((bf16[64,1536,16]{1,2,0:T(8,128)(2,1)}), bf16[64,1536,16]{1,2,0:T(8,128)(2,1)S(1)}, u32[]{:S(2)}, u32[]{:S(2)}) async-start(bf16[64,1536,16]{1,2,0:T(8,128)(2,1)} %broadcast_select_fusion.1), calls=%async_computation.3 | async-start | bytes 6291456 | tf_op jit(solution)/shard_map/all_to_all | solution.py:67
  382.4 84.8 %all-gather.7.cloned.1.call-start = ((), (), s32[]{:S(2)}) async-start(), calls=%async_computation.7 | async-start | bytes 1966080 | tf_op jit(solution)/shard_map/all_gather | solution.py:101
  410.6 80.2 %all-gather.9.cloned.1.call-start = ((), (), s32[]{:S(2)}) async-start(), calls=%async_computation.8 | async-start | bytes 1966080 | tf_op jit(solution)/shard_map/all_gather | solution.py:101
  474.6 38.9 %all-to-all-start.4 = ((bf16[256,1,1,1,2,1024]{5,4,3,2,1,0:T(2,128)(2,1)}), bf16[256,1,1,1,2,1024]{5,4,3,2,1,0:T(2,128)(2,1)}, u32[]{:S(2)}, u32[]{:S(2)}) async-start(bf16[256,1,1,1,2,1024]{5,4,3,2,1,0:T(2,128)(2,1)} %copy.188), calls=%async_computation.4 | async-start | bytes 2097152 | tf_op jit(solution)/shard_map/all_to_all | solution.py:28
  495.1 25.3 %copy-start.3 = (f32[2,8,8]{2,1,0:T(8,128)S(1)}, f32[2,8,8]{2,1,0:T(8,128)}, u32[]{:S(2)}) copy-start(f32[2,8,8]{2,1,0:T(8,128)} %param.8) | copy-start | bytes 1540
  496.2 60.4 %copy-start.1 = (bf16[64,1536,16]{1,2,0:T(8,128)(2,1)S(1)}, bf16[64,1536,16]{1,2,0:T(8,128)(2,1)}, u32[]{:S(2)}) copy-start(bf16[64,1536,16]{1,2,0:T(8,128)(2,1)} %param.11) | copy-start | bytes 9437188
  513.5 37.2 %all-to-all-start.6 = ((bf16[256,1,1,1,2,1024]{5,4,3,2,1,0:T(2,128)(2,1)}), bf16[256,1,1,1,2,1024]{5,4,3,2,1,0:T(2,128)(2,1)}, u32[]{:S(2)}, u32[]{:S(2)}) async-start(bf16[256,1,1,1,2,1024]{5,4,3,2,1,0:T(2,128)(2,1)} %copy.194), calls=%async_computation.6 | async-start | bytes 2097152 | tf_op jit(solution)/shard_map/all_to_all | solution.py:28
Sparse Core Ops, SparseCore 0:
  93.9 51.7 all-gather.10
  276.2 81.6 all-gather.12
  410.7 27.9 all-gather.6
  464.8 25.9 all-gather.8
